TPU v7x, 32 devices: a whole 2x2x4 slice. The times are simulated.
32 devices in a mesh: blk: 8 (over y, x, core), group: 4 (over z).
Axes of the slice: x: 2, y: 2, z: 4, core: 2. Of those that a mesh axis runs over, the one named last changes fastest.
Arguments:
- image_embed: bfloat16 [2048, 1152], P(('blk', 'group')), may hold values from -6 to 6
- caption_vectors: bfloat16 [16384, 1152], P(('blk', 'group')), may hold values from -6 to 6
- caption_counts: int32 [2048], replicated, may hold values from 1 to 8, as said below
- natural_log_multiplier: float32 [1], replicated, may hold values from 1.5 to 2.5
- match_odds_offset: float32 [1], replicated, may hold values from -6 to -4
Outputs:
- image_grad: float32 [2048, 1152], P(('blk', 'group'))
- caption_grad: float32 [16384, 1152], P(('blk', 'group'))
Inputs may be any that keep to these rules, and one draw needn't show every extreme that they name: Images are numbered as in caption_counts, 64 to a device, devices in the order of blk then group. Local image k of the device with blk index b < 4 and group index g and local image k of the device with blk index b + 4 and group index g have counts that sum to 9. On at least one device all 64 images have 8 captions.
All inputs are finite; a program needn't handle non-finite values.
Results may differ from a plain program's by a relative error of at most 0.0028.
Values may be sent and summed in bfloat16 or wider, within the bound.
A program may use at most 64 MiB of HBM per device.

v0:
```python
import jax
import jax.numpy as jnp
from jax import lax
from jax.sharding import PartitionSpec as P

EPSILON = 1e-06


def swapped(value, axis, stride):
    return lax.ppermute(value, axis, [(i, i ^ 1 << stride) for i in range(lax.axis_size(axis))])


def shifted(block, axis, distance):
    devices = range(lax.axis_size(axis))
    route = [((i - distance) % len(devices), i) for i in devices]
    return lax.ppermute(block, axis, route)


def normalize(embed_rows):
    values = embed_rows.astype(jnp.float32)
    inverse = lax.rsqrt(jnp.sum(values * values, axis=1, keepdims=True) + EPSILON)
    return (values * inverse, inverse)


def slot_owners(device_counts, first_image, slot_count):
    running_end = jnp.cumsum(device_counts)
    position = lax.broadcasted_iota(jnp.int32, (slot_count, device_counts.shape[0]), 0)
    local_index = jnp.sum((running_end[None, :] <= position).astype(jnp.int32), axis=1)
    present_entry_flags = position[:, 0] < running_end[-1]
    return jnp.where(present_entry_flags, first_image + local_index, -1)


def balanced_pick(own_total, slot_count, kept_rows):
    position = lax.iota(jnp.int32, kept_rows)
    return jnp.where(position < own_total, position, slot_count + position - own_total)


def shards(image_embed, caption_vectors, caption_counts, natural_log_multiplier, match_odds_offset):
    image_count = image_embed.shape[0]
    slot_count = caption_vectors.shape[0]
    kept_rows = 9 * image_count // 2
    blocks = lax.axis_size("blk")
    groups = lax.axis_size("group")
    pair_bit = blocks.bit_length() - 2
    blk_index = lax.axis_index("blk")
    group_index = lax.axis_index("group")
    odds_sharpness_factor = jnp.exp(natural_log_multiplier[0])
    bias_value = match_odds_offset[0]
    image_unit, image_inverse = normalize(image_embed)
    caption_unit, caption_inverse = normalize(caption_vectors)
    caption_low = caption_unit.astype(jnp.bfloat16)
    gathered = lax.all_gather(image_unit.astype(jnp.bfloat16), "blk", axis=0, tiled=True)
    column_pos = lax.iota(jnp.int32, blocks * image_count)
    column_ids = (
        column_pos // image_count * groups + group_index
    ) * image_count + column_pos % image_count

    def device_counts(device_id):
        return lax.dynamic_slice_in_dim(caption_counts, device_id * image_count, image_count)

    def source_owners(source_group):
        own_id = blk_index * groups + source_group
        own_counts = device_counts(own_id)
        own_owner = slot_owners(own_counts, own_id * image_count, slot_count)
        partner_id = (blk_index ^ blocks // 2) * groups + source_group
        partner_owner = slot_owners(device_counts(partner_id), partner_id * image_count, slot_count)
        own_total = jnp.sum(own_counts)
        joined = jnp.concatenate([own_owner, partner_owner[kept_rows:]])
        return jnp.take(joined, balanced_pick(own_total, slot_count, kept_rows))

    owner_table = jax.vmap(source_owners)(lax.iota(jnp.int32, groups))
    home_id = blk_index * groups + group_index
    home_counts = device_counts(home_id)
    home_total = jnp.sum(home_counts)
    home_owner = slot_owners(home_counts, home_id * image_count, slot_count)
    partner_tail = swapped(caption_low[kept_rows:], "blk", pair_bit)
    moving_rows = jnp.take(
        jnp.concatenate([caption_low, partner_tail], axis=0),
        balanced_pick(home_total, slot_count, kept_rows),
        axis=0,
    )

    def row_terms(moving, grad_rows, owners, image_acc):
        similarity_matrix = (
            odds_sharpness_factor
            * lax.dot_general(
                moving, gathered, (((1,), (1,)), ((), ())), preferred_element_type=jnp.float32
            )
            + bias_value
        )
        match_target_signs = jnp.where(owners[:, None] == column_ids[None, :], 1.0, -1.0)
        present_entry_flags = (owners >= 0)[:, None]
        oriented_similarity_gap = match_target_signs * similarity_matrix
        match_loss_factors = jnp.where(
            present_entry_flags,
            odds_sharpness_factor
            * (-match_target_signs * jax.nn.sigmoid(-oriented_similarity_gap)),
            0.0,
        ).astype(jnp.bfloat16)
        grad_rows = grad_rows + jnp.dot(
            match_loss_factors, gathered, preferred_element_type=jnp.float32
        )
        image_acc = image_acc + lax.dot_general(
            match_loss_factors, moving, (((0,), (0,)), ((), ())), preferred_element_type=jnp.float32
        )
        return (grad_rows, image_acc)

    def owners_from(source_group):
        return lax.dynamic_index_in_dim(owner_table, source_group % groups, 0, keepdims=False)

    row_count = moving_rows.shape[0]
    image_acc = jnp.zeros(gathered.shape, jnp.float32)

    def pass_ahead(grad_rows):
        return shifted(grad_rows, "group", 1)

    grad_rows, image_acc = row_terms(
        moving_rows,
        jnp.zeros((row_count, gathered.shape[1]), jnp.float32),
        owners_from(group_index),
        image_acc,
    )

    def turn_step(step_index, loop_state):
        moving, grad_rows, image_acc = loop_state
        moving = shifted(moving, "group", 1)
        grad_rows = pass_ahead(grad_rows)
        grad_rows, image_acc = row_terms(
            moving, grad_rows, owners_from(group_index - step_index), image_acc
        )
        return (moving, grad_rows, image_acc)

    loop_state = lax.fori_loop(1, groups, turn_step, (moving_rows, grad_rows, image_acc))
    grad_total = pass_ahead(loop_state[1])
    image_acc = loop_state[2]
    image_sum = lax.psum_scatter(image_acc, "blk", scatter_dimension=0, tiled=True)
    image_grad = (
        image_sum - image_unit * jnp.sum(image_unit * image_sum, axis=1, keepdims=True)
    ) * image_inverse
    back_pos = home_total + lax.iota(jnp.int32, slot_count - kept_rows)
    back_rows = jnp.where(
        (back_pos < kept_rows)[:, None],
        jnp.take(grad_total, jnp.minimum(back_pos, kept_rows - 1), axis=0),
        0.0,
    )
    returned = swapped(back_rows, "blk", pair_bit)
    head_rows = jnp.where((lax.iota(jnp.int32, kept_rows) < home_total)[:, None], grad_total, 0.0)
    slot_grads = jnp.concatenate([head_rows, returned], axis=0)
    caption_grad = jnp.where(
        (home_owner >= 0)[:, None],
        (slot_grads - caption_unit * jnp.sum(caption_unit * slot_grads, axis=1, keepdims=True))
        * caption_inverse,
        0.0,
    )
    return (image_grad, caption_grad)


def solution(mesh):
    placed = (P(("blk", "group"), None), P(("blk", "group"), None), P(), P(), P())
    return jax.shard_map(
        shards,
        mesh=mesh,
        in_specs=placed,
        out_specs=(P(("blk", "group"), None), P(("blk", "group"), None)),
        check_vma=False,
    )
```

profile of v0, /device:TPU:0, one launch (start us, length us, event | category | flops | bytes accessed | tf_op | source)
XLA Modules:
  0.0 274.8 jit_solution(6474063916354677370)
XLA Ops:
  9.2 3.1 %collective-permute-start.2 = (bf16[224,1152]{1,0:T(8,128)(2,1)S(1)}, bf16[224,1152]{1,0:T(8,128)(2,1)S(1)}, u32[]{:S(2)}, u32[]{:S(2)}) collective-permute-start(bf16[224,1152]{1,0:T(8,128)(2,1)S(1)} %slice.49), channel_id=1, source_target_pairs={{0,16},{4,20},{8,24},{12,28},{16,0},{20,4},{24,8},{28,12},{1,17},{... | collective-permute-start | bytes 1548296 | tf_op jit(solution)/shard_map/ppermute | solution.py:10
  13.3 8.7 %while.23 = (s32[]{:T(128)}, s32[2048]{0:T(1024)}, s32[4,1]{0,1:T(1,128)S(1)}, s32[4,64]{1,0:T(4,128)S(1)}, s32[]{:T(128)}, /*index=5*/s32[]{:T(128)}) while((s32[]{:T(128)}, s32[2048]{0:T(1024)}, s32[4,1]{0,1:T(1,128)S(1)}, s32[4,64]{1,0:T(4,128)S(1)}, s32[]{:T(128)}, /*index=5*/s32[]{:T(128)}) %tuple.73), condition=%wide.while_cond, body=%wide.while_body.sunk | while | flops 2 | bytes 1113 | solution.py:59
  22.6 8.6 %while.24 = (s32[]{:T(128)}, s32[2048]{0:T(1024)}, s32[4,1]{0,1:T(1,128)S(1)}, s32[4,64]{1,0:T(4,128)S(1)}, s32[]{:T(128)}, /*index=5*/s32[]{:T(128)}) while((s32[]{:T(128)}, s32[2048]{0:T(1024)}, s32[4,1]{0,1:T(1,128)S(1)}, s32[4,64]{1,0:T(4,128)S(1)}, s32[]{:T(128)}, /*index=5*/s32[]{:T(128)}) %tuple.84), condition=%wide.while_cond.1, body=%wide.while_body.1.sunk | while | flops 2 | bytes 1113 | solution.py:59
  32.3 9.8 %gather_fusion.2 = s32[1152]{0:T(1024)S(1)} fusion(s32[4,736]{1,0:T(4,128)S(1)} %pad_add_fusion, s32[1152]{0:T(1024)S(1)} %reshape.359), kind=kCustom, calls=%fused_computation.2 | custom fusion | bytes 18432 | tf_op jit(solution)/shard_map/vmap(jit(_take))/gather | solution.py:69
  43.7 2.0 dynamic-slice_bitcast_fusion.2
  48.8 2.2 gather_fusion
  52.0 2.0 fusion.38
  54.1 2.0 fusion.64
  57.7 147.2 %while.25 = (s32[]{:T(128)}, bf16[288,1152]{1,0:T(8,128)(2,1)}, f32[288,1152]{1,0:T(8,128)}, f32[512,1152]{1,0:T(8,128)S(1)}, s32[]{:T(128)}, /*index=5*/s32[4,2...) while((s32[]{:T(128)}, bf16[288,1152]{1,0:T(8,128)(2,1)}, ...), condition=%wide.region_9.10_spmd.clone.clone, body=%wide.region_8.9_spmd.clone.clone.sunk | while | flops 1021915456 | bytes 25961940 | solution.py:133
  60.9 16.6 %collective-permute-done = bf16[288,1152]{1,0:T(8,128)(2,1)S(1)} collective-permute-done((bf16[288,1152]{1,0:T(8,128)(2,1)}, bf16[288,1152]{1,0:T(8,128)(2,1)S(1)}, u32[]{:S(2)}, u32[]{:S(2)}) %collective-permute-start) | collective-permute-done | bytes 663584 | tf_op jit(solution)/shard_map/while/body/eval_jaxpr/ppermute | solution.py:16
  78.4 2.7 fusion.92
  82.1 22.6 %collective-permute-done.1 = f32[288,1152]{1,0:T(8,128)} collective-permute-done((f32[288,1152]{1,0:T(8,128)}, f32[288,1152]{1,0:T(8,128)}, u32[]{:S(2)}, u32[]{:S(2)}) %collective-permute-start.1) | collective-permute-done | bytes 1327136 | tf_op jit(solution)/shard_map/while/body/eval_jaxpr/ppermute | solution.py:16
  104.7 2.9 %convolution_add_fusion.4 = f32[288,1152]{1,0:T(8,128)} fusion(f32[288,1152]{1,0:T(8,128)} %collective-permute-done.1, bf16[288,512]{1,0:T(8,128)(2,1)S(1)} %fusion.92, bf16[512,1152]{1,0:T(8,128)(2,1)S(1)} %copy-done.2), kind=kOutput, calls=%fused_computation.9.clone.1 | convolution fusion | flops 340070400 | bytes 4128768 | tf_op jit(solution)/shard_map/while/body/eval_jaxpr/dot_general | solution.py:100
  109.0 18.4 %collective-permute-done = bf16[288,1152]{1,0:T(8,128)(2,1)S(1)} collective-permute-done((bf16[288,1152]{1,0:T(8,128)(2,1)}, bf16[288,1152]{1,0:T(8,128)(2,1)S(1)}, u32[]{:S(2)}, u32[]{:S(2)}) %collective-permute-start) | collective-permute-done | bytes 663584 | tf_op jit(solution)/shard_map/while/body/eval_jaxpr/ppermute | solution.py:16
  128.3 2.7 fusion.92
  132.0 21.7 %collective-permute-done.1 = f32[288,1152]{1,0:T(8,128)} collective-permute-done((f32[288,1152]{1,0:T(8,128)}, f32[288,1152]{1,0:T(8,128)}, u32[]{:S(2)}, u32[]{:S(2)}) %collective-permute-start.1) | collective-permute-done | bytes 1327136 | tf_op jit(solution)/shard_map/while/body/eval_jaxpr/ppermute | solution.py:16
  153.8 2.9 %convolution_add_fusion.4 = f32[288,1152]{1,0:T(8,128)} fusion(f32[288,1152]{1,0:T(8,128)} %collective-permute-done.1, bf16[288,512]{1,0:T(8,128)(2,1)S(1)} %fusion.92, bf16[512,1152]{1,0:T(8,128)(2,1)S(1)} %copy-done.2), kind=kOutput, calls=%fused_computation.9.clone.1 | convolution fusion | flops 340070400 | bytes 4128768 | tf_op jit(solution)/shard_map/while/body/eval_jaxpr/dot_general | solution.py:100
  156.8 19.7 %collective-permute-done = bf16[288,1152]{1,0:T(8,128)(2,1)S(1)} collective-permute-done((bf16[288,1152]{1,0:T(8,128)(2,1)}, bf16[288,1152]{1,0:T(8,128)(2,1)S(1)}, u32[]{:S(2)}, u32[]{:S(2)}) %collective-permute-start) | collective-permute-done | bytes 663584 | tf_op jit(solution)/shard_map/while/body/eval_jaxpr/ppermute | solution.py:16
  177.4 2.7 fusion.92
  181.1 20.9 %collective-permute-done.1 = f32[288,1152]{1,0:T(8,128)} collective-permute-done((f32[288,1152]{1,0:T(8,128)}, f32[288,1152]{1,0:T(8,128)}, u32[]{:S(2)}, u32[]{:S(2)}) %collective-permute-start.1) | collective-permute-done | bytes 1327136 | tf_op jit(solution)/shard_map/while/body/eval_jaxpr/ppermute | solution.py:16
  202.0 2.9 %convolution_add_fusion.4 = f32[288,1152]{1,0:T(8,128)} fusion(f32[288,1152]{1,0:T(8,128)} %collective-permute-done.1, bf16[288,512]{1,0:T(8,128)(2,1)S(1)} %fusion.92, bf16[512,1152]{1,0:T(8,128)(2,1)S(1)} %copy-done.2), kind=kOutput, calls=%fused_computation.9.clone.1 | convolution fusion | flops 340070400 | bytes 4128768 | tf_op jit(solution)/shard_map/while/body/eval_jaxpr/dot_general | solution.py:100
  207.6 27.5 %collective-permute-done.3 = f32[288,1152]{1,0:T(8,128)} collective-permute-done((f32[288,1152]{1,0:T(8,128)}, f32[288,1152]{1,0:T(8,128)}, u32[]{:S(2)}, u32[]{:S(2)}) %collective-permute-start.3) | collective-permute-done | bytes 1327136 | tf_op jit(solution)/shard_map/ppermute | solution.py:16
  235.1 2.9 %gather_fusion.1 = f32[224,1152]{1,0:T(8,128)S(1)} fusion(f32[288,1152]{1,0:T(8,128)} %collective-permute-done.3, s32[1024]{0:T(1024)S(1)} %pad_clamp_fusion), kind=kCustom, calls=%fused_computation.1 | custom fusion | bytes 2065280 | tf_op jit(solution)/shard_map/jit(_take)/gather | solution.py:143
  243.7 18.9 %collective-permute-done.4 = f32[224,1152]{1,0:T(8,128)S(1)} collective-permute-done((f32[224,1152]{1,0:T(8,128)S(1)}, f32[224,1152]{1,0:T(8,128)S(1)}, u32[]{:S(2)}, u32[]{:S(2)}) %collective-permute-start.4) | collective-permute-done | bytes 1032224 | tf_op jit(solution)/shard_map/ppermute | solution.py:10
  (146 shorter events, 51.8 us)
Async XLA Ops:
  7.2 44.0 %all-gather.2.cloned.1.call-start = ((), (), s32[]{:S(2)}) async-start(), calls=%async_computation.1 | async-start | bytes 1327104 | tf_op jit(solution)/shard_map/all_gather | solution.py:52
  8.9 3.4 %copy-start.6 = (bf16[64,1152]{1,0:T(8,128)(2,1)S(1)}, bf16[64,1152]{1,0:T(8,128)(2,1)}, u32[]{:S(2)}) copy-start(bf16[64,1152]{1,0:T(8,128)(2,1)} %param.7) | copy-start | bytes 442372
  9.2 39.4 %collective-permute-start.2 = (bf16[224,1152]{1,0:T(8,128)(2,1)S(1)}, bf16[224,1152]{1,0:T(8,128)(2,1)S(1)}, u32[]{:S(2)}, u32[]{:S(2)}) collective-permute-start(bf16[224,1152]{1,0:T(8,128)(2,1)S(1)} %slice.49), channel_id=1, source_target_pairs={{0,16},{4,20},{8,24},{12,28},{16,0},{20,4},{24,8},{28,12},{1,17},{... | collective-permute-start | bytes 1548296 | tf_op jit(solution)/shard_map/ppermute | solution.py:10
  12.4 18.7 %copy-start.10 = (f32[64]{0:T(128)}, f32[64]{0:T(128)S(1)}, u32[]{:S(2)}) copy-start(f32[64]{0:T(128)S(1)} %add_rsqrt_fusion.1) | copy-start | bytes 772
  13.2 251.8 %reduce-scatter.2.cloned.1.call-start = ((), (), s32[]{:S(2)}) async-start(), calls=%async_computation.2 | async-start | bytes 2654208 | tf_op jit(solution)/shard_map/reduce_scatter | solution.py:136
  43.6 5.0 %copy-start.8 = (s32[288]{0:T(512)}, s32[288]{0:T(512)S(1)}, u32[]{:S(2)}) copy-start(s32[288]{0:T(512)S(1)} %dynamic-slice_reduce_fusion.1) | copy-start | bytes 3460
  48.8 2.2 copy-start.14
  48.8 3.2 %copy-start.9 = (s32[288]{0:T(512)S(1)}, s32[288]{0:T(512)}, u32[]{:S(2)}) copy-start(s32[288]{0:T(512)} %copy-done.8) | copy-start | bytes 3460
  48.8 3.2 %copy-start.13 = (s32[512]{0:T(512)S(1)}, s32[512]{0:T(512)}, u32[]{:S(2)}) copy-start(s32[512]{0:T(512)} %fusion.57) | copy-start | bytes 6148
  48.8 3.2 %copy-start.15 = (pred[288]{0:T(512)(128)(4,1)S(1)}, pred[288]{0:T(512)(128)(4,1)}, u32[]{:S(2)}) copy-start(pred[288]{0:T(512)(128)(4,1)} %broadcast_compare_fusion.1) | copy-start | bytes 868
  54.1 2.1 copy-start.1
  57.7 19.8 %collective-permute-start = (bf16[288,1152]{1,0:T(8,128)(2,1)}, bf16[288,1152]{1,0:T(8,128)(2,1)S(1)}, u32[]{:S(2)}, u32[]{:S(2)}) collective-permute-start(bf16[288,1152]{1,0:T(8,128)(2,1)} %get-tuple-element.502), channel_id=1, source_target_pairs={{3,0},{0,1},{1,2},{2,3},{7,4},{4,5},{5,6},{6,7},{11,8},{8,9},{9,10... | collective-permute-start | bytes 1990664 | tf_op jit(solution)/shard_map/while/body/eval_jaxpr/ppermute | solution.py:16
  59.3 45.4 %collective-permute-start.1 = (f32[288,1152]{1,0:T(8,128)}, f32[288,1152]{1,0:T(8,128)}, u32[]{:S(2)}, u32[]{:S(2)}) collective-permute-start(f32[288,1152]{1,0:T(8,128)} %get-tuple-element.503), channel_id=1, source_target_pairs={{3,0},{0,1},{1,2},{2,3},{7,4},{4,5},{5,6},{6,7},{11,8},{8,9},{9,10... | collective-permute-start | bytes 3981320 | tf_op jit(solution)/shard_map/while/body/eval_jaxpr/ppermute | solution.py:16
  81.1 23.7 %copy-start.2 = (bf16[512,1152]{1,0:T(8,128)(2,1)S(1)}, bf16[512,1152]{1,0:T(8,128)(2,1)}, u32[]{:S(2)}) copy-start(bf16[512,1152]{1,0:T(8,128)(2,1)} %get-tuple-element.521) | copy-start | bytes 3538948 | tf_op jit(solution)/shard_map/while
  107.7 19.8 %collective-permute-start = (bf16[288,1152]{1,0:T(8,128)(2,1)}, bf16[288,1152]{1,0:T(8,128)(2,1)S(1)}, u32[]{:S(2)}, u32[]{:S(2)}) collective-permute-start(bf16[288,1152]{1,0:T(8,128)(2,1)} %get-tuple-element.502), channel_id=1, source_target_pairs={{3,0},{0,1},{1,2},{2,3},{7,4},{4,5},{5,6},{6,7},{11,8},{8,9},{9,10... | collective-permute-start | bytes 1990664 | tf_op jit(solution)/shard_map/while/body/eval_jaxpr/ppermute | solution.py:16
  107.7 46.1 %collective-permute-start.1 = (f32[288,1152]{1,0:T(8,128)}, f32[288,1152]{1,0:T(8,128)}, u32[]{:S(2)}, u32[]{:S(2)}) collective-permute-start(f32[288,1152]{1,0:T(8,128)} %get-tuple-element.503), channel_id=1, source_target_pairs={{3,0},{0,1},{1,2},{2,3},{7,4},{4,5},{5,6},{6,7},{11,8},{8,9},{9,10... | collective-permute-start | bytes 3981320 | tf_op jit(solution)/shard_map/while/body/eval_jaxpr/ppermute | solution.py:16
  131.0 22.8 %copy-start.2 = (bf16[512,1152]{1,0:T(8,128)(2,1)S(1)}, bf16[512,1152]{1,0:T(8,128)(2,1)}, u32[]{:S(2)}) copy-start(bf16[512,1152]{1,0:T(8,128)(2,1)} %get-tuple-element.521) | copy-start | bytes 3538948 | tf_op jit(solution)/shard_map/while
  156.7 19.8 %collective-permute-start = (bf16[288,1152]{1,0:T(8,128)(2,1)}, bf16[288,1152]{1,0:T(8,128)(2,1)S(1)}, u32[]{:S(2)}, u32[]{:S(2)}) collective-permute-start(bf16[288,1152]{1,0:T(8,128)(2,1)} %get-tuple-element.502), channel_id=1, source_target_pairs={{3,0},{0,1},{1,2},{2,3},{7,4},{4,5},{5,6},{6,7},{11,8},{8,9},{9,10... | collective-permute-start | bytes 1990664 | tf_op jit(solution)/shard_map/while/body/eval_jaxpr/ppermute | solution.py:16
  156.7 45.3 %collective-permute-start.1 = (f32[288,1152]{1,0:T(8,128)}, f32[288,1152]{1,0:T(8,128)}, u32[]{:S(2)}, u32[]{:S(2)}) collective-permute-start(f32[288,1152]{1,0:T(8,128)} %get-tuple-element.503), channel_id=1, source_target_pairs={{3,0},{0,1},{1,2},{2,3},{7,4},{4,5},{5,6},{6,7},{11,8},{8,9},{9,10... | collective-permute-start | bytes 3981320 | tf_op jit(solution)/shard_map/while/body/eval_jaxpr/ppermute | solution.py:16
  180.0 21.9 %copy-start.2 = (bf16[512,1152]{1,0:T(8,128)(2,1)S(1)}, bf16[512,1152]{1,0:T(8,128)(2,1)}, u32[]{:S(2)}) copy-start(bf16[512,1152]{1,0:T(8,128)(2,1)} %get-tuple-element.521) | copy-start | bytes 3538948 | tf_op jit(solution)/shard_map/while
  204.9 30.2 %collective-permute-start.3 = (f32[288,1152]{1,0:T(8,128)}, f32[288,1152]{1,0:T(8,128)}, u32[]{:S(2)}, u32[]{:S(2)}) collective-permute-start(f32[288,1152]{1,0:T(8,128)} %get-tuple-element.247), channel_id=1, source_target_pairs={{3,0},{0,1},{1,2},{2,3},{7,4},{4,5},{5,6},{6,7},{11,8},{8,9},{9,10... | collective-permute-start | bytes 3981320 | tf_op jit(solution)/shard_map/ppermute | solution.py:16
  238.0 2.6 copy-start.12
  238.2 24.3 %copy-start.4 = (bf16[512,1152]{1,0:T(8,128)(2,1)S(1)}, bf16[512,1152]{1,0:T(8,128)(2,1)}, u32[]{:S(2)}) copy-start(bf16[512,1152]{1,0:T(8,128)(2,1)} %param.8) | copy-start | bytes 3538948
  238.2 24.3 %collective-permute-start.4 = (f32[224,1152]{1,0:T(8,128)S(1)}, f32[224,1152]{1,0:T(8,128)S(1)}, u32[]{:S(2)}, u32[]{:S(2)}) collective-permute-start(f32[224,1152]{1,0:T(8,128)S(1)} %select_select_fusion), channel_id=1, source_target_pairs={{0,16},{4,20},{8,24},{12,28},{16,0},{20,4},{24,8},{28,12},{1,17},{... | collective-permute-start | bytes 3096584 | tf_op jit(solution)/shard_map/ppermute | solution.py:10
  (5 other events, 7.9 us)
Sparse Core Ops, SparseCore 0:
  13.3 25.4 all-gather.1
  206.5 47.2 reduce-scatter.1
where the time goes:
time: 276 us; the launch traced here: 275 us
  waiting for transfers between devices  166 us (60%)
  local copies, waits for them, and re-layouts  38.3 us (14%)
  matrix products  25.6 us (9%)
  other arithmetic  19.3 us (7%)
  between operations  15.7 us (6%)
  starting transfers between devices  9.31 us (3%)
    ppermute x7, waiting for transfers between devices, shifted(): return lax.ppermute(block, axis, route)  147 us
    ppermute x2, waiting for transfers between devices, swapped(): lax.ppermute(value, axis, [(i, i ^ 1 << stride) for i in range(lax.axis_s...  18.9 us
    gather x24, local copies, waits for them, and re-layouts  17.2 us
    dot_general x4, matrix products, row_terms(): jnp.dot(match_loss_factors, gathered, preferred_element_type=jnp.float32)  10.4 us
    dot_general x4, matrix products, row_terms(): lax.dot_general(moving, gathered, (((1,), (1,)), ((), ())), preferred_ele...  10 us
    gather x3, local copies, waits for them, and re-layouts, source_owners(): return jnp.take(joined, balanced_pick(own_total, slot_count, kept_rows))  9.97 us
  transfers between devices with their start and end apart: 11, of which 8 were waited for; matrix products, arithmetic and copies ran while one was open for 22% of the time, Pallas kernels for 0%

commit v1 on v0

v1 whole, which is shorter than its diff:
```python
import functools

import jax
import jax.numpy as jnp
from jax import lax
from jax.experimental import pallas as pl
from jax.experimental.pallas import tpu as pltpu
from jax.sharding import PartitionSpec as P

EPSILON = 1e-06
MESH = pl.DeviceIdType.MESH
ROWS = 256


def normalize(embed_rows):
    values = embed_rows.astype(jnp.float32)
    inverse = lax.rsqrt(jnp.sum(values * values, axis=1, keepdims=True) + EPSILON)
    return (values * inverse, inverse)


def flipped(index, mask):
    bit = 1
    while bit <= mask:
        if mask & bit:
            index = index + bit - 2 * bit * ((index // bit) % 2)
        bit *= 2
    return index


def kernel(
    chips, groups,
    image_ref, caption_ref, bounds_ref, totals_ref, scalars_ref,
    image_grad_ref, caption_grad_ref,
    images, captions, caption_inverse, caption_sum, own_partial, partial,
    out_partial, in_partial, out_sum, in_sum, out_caption, in_caption,
    line_send, line_recv, plane_send, plane_recv, part_send, part_recv,
    sum_send, sum_recv, pair_send, pair_recv,
):
    blk = lax.axis_index("blk")
    group = lax.axis_index("group")
    core = blk % 2
    chip = blk // 2
    image_count = image_ref.shape[0]
    slots = caption_ref.shape[0]
    columns = groups * image_count
    masks = sorted(range(1, chips), key=lambda m: (bin(m).count("1"), m))
    temperature = scalars_ref[0]
    bias = scalars_ref[1]

    def plane_peer(mask):
        return (flipped(chip, mask) * 2 + core, group)

    def line_peer(distance):
        return (blk, (group + distance) % groups)

    pair_peer = (chip * 2 + 1 - core, group)

    barrier = pltpu.get_barrier_semaphore()
    peers = [pair_peer]
    peers += [plane_peer(m) for m in masks]
    peers += [line_peer(d) for d in range(1, groups)]
    for peer in peers:
        pl.semaphore_signal(barrier, inc=1, device_id=peer, device_id_type=MESH)
    image_unit, image_inverse = normalize(image_ref[...])
    images[chip, group] = image_unit.astype(jnp.bfloat16)
    pl.semaphore_wait(barrier, len(peers))

    def remote(source, target, send, recv, peer):
        return pltpu.make_async_remote_copy(
            src_ref=source, dst_ref=target, send_sem=send, recv_sem=recv,
            device_id=peer, device_id_type=MESH,
        )

    def line_copy(d):
        here = images.at[chip, group]
        return remote(here, here, line_send.at[d - 1], line_recv.at[d - 1], line_peer(d))

    def plane_copy(mask, d):
        here = images.at[chip, (group - d + groups) % groups]
        return remote(
            here, here, plane_send.at[mask - 1, d], plane_recv.at[mask - 1, d], plane_peer(mask)
        )

    def part_copy(mask, unit):
        return remote(
            out_partial.at[mask - 1, unit], in_partial.at[mask - 1, unit],
            part_send.at[mask - 1, unit], part_recv.at[mask - 1, unit], plane_peer(mask),
        )

    def sum_copy(d):
        return remote(
            out_sum.at[d - 1], in_sum.at[d - 1], sum_send.at[d - 1], sum_recv.at[d - 1],
            line_peer(d),
        )

    near = [m for m in masks if bin(m).count("1") == 1]
    far = [m for m in masks if m not in near]
    for d in range(1, groups):
        line_copy(d).start()
    for m in masks:
        plane_copy(m, 0).start()

    step = min(slots, 128)

    @pl.loop(0, slots // step)
    def _(i):
        rows = pl.ds(pl.multiple_of(i * step, step), step)
        unit, inverse = normalize(caption_ref[rows, :])
        captions[0, rows, :] = unit.astype(jnp.bfloat16)
        caption_inverse[rows, :] = inverse

    caption_copy = remote(
        captions.at[0], captions.at[1], pair_send.at[0], pair_recv.at[0], pair_peer
    )
    caption_copy.start()
    for d in range(1, groups):
        line_copy(d).wait_recv()
        for m in near:
            plane_copy(m, d).start()
    for d in range(1, groups):
        for m in far:
            plane_copy(m, d).start()
    caption_copy.wait_recv()

    blocks = slots // ROWS

    def chunk(source_chip, target, own):
        target[...] = jnp.zeros_like(target)

        @pl.loop(0, 2 * blocks)
        def _(i):
            half = i // blocks
            offset = pl.multiple_of((i % blocks) * ROWS, ROWS)
            rows = pl.ds(offset, ROWS)
            block = captions[half, rows, :]
            picked = images[source_chip].reshape(columns, -1)
            scores = temperature * lax.dot_general(
                block, picked, (((1,), (1,)), ((), ())), preferred_element_type=jnp.float32
            ) + bias
            position = offset + lax.broadcasted_iota(jnp.int32, scores.shape, 0)
            chance = 1.0 / (1.0 + jnp.exp(-scores))
            if own:
                shifted = position + half * slots
                match = (shifted >= bounds_ref[0:1, :]) & (shifted < bounds_ref[1:2, :])
                chance = jnp.where(match, -1.0 / (1.0 + jnp.exp(scores)), chance)
            weight = jnp.where(position < totals_ref[half], temperature * chance, 0.0)
            weight = weight.astype(jnp.bfloat16)
            gained = jnp.dot(weight, picked, preferred_element_type=jnp.float32)
            if own:
                caption_sum[half, rows, :] = gained
            else:
                caption_sum[half, rows, :] += gained
            target[...] += lax.dot_general(
                weight, block, (((0,), (0,)), ((), ())), preferred_element_type=jnp.float32
            )

    chunk(chip, own_partial, True)
    for m in masks:
        for d in range(groups):
            plane_copy(m, d).wait_recv()
        chunk(flipped(chip, m), partial, False)
        for unit in range(groups):
            rows = slice(unit * image_count, (unit + 1) * image_count)
            out_partial[m - 1, unit] = partial[rows, :].astype(jnp.bfloat16)
            part_copy(m, unit).start()

    out_caption[...] = caption_sum[1].astype(jnp.bfloat16)
    back_copy = remote(out_caption, in_caption, pair_send.at[1], pair_recv.at[1], pair_peer)
    back_copy.start()

    def column_total(unit):
        rows = pl.ds(pl.multiple_of(unit * image_count, image_count), image_count)
        total = own_partial[rows, :]
        for m in masks:
            part_copy(m, unit).wait_recv()
            total = total + in_partial[m - 1, unit].astype(jnp.float32)
        return total

    back_copy.wait_recv()

    @pl.loop(0, slots // step)
    def _(i):
        offset = pl.multiple_of(i * step, step)
        rows = pl.ds(offset, step)
        inverse = caption_inverse[rows, :]
        unit = caption_ref[rows, :].astype(jnp.float32) * inverse
        total = caption_sum[0, rows, :] + in_caption[rows, :].astype(jnp.float32)
        grad = (total - unit * jnp.sum(unit * total, axis=1, keepdims=True)) * inverse
        position = offset + lax.broadcasted_iota(jnp.int32, grad.shape, 0)
        caption_grad_ref[rows, :] = jnp.where(position < totals_ref[0], grad, 0.0)

    for d in range(1, groups):
        out_sum[d - 1] = column_total((group + d) % groups).astype(jnp.bfloat16)
        sum_copy(d).start()
    image_sum = column_total(group)
    for d in range(1, groups):
        sum_copy(d).wait_recv()
        image_sum = image_sum + in_sum[d - 1].astype(jnp.float32)
    image_unit, image_inverse = normalize(image_ref[...])
    image_grad_ref[...] = (
        image_sum - image_unit * jnp.sum(image_unit * image_sum, axis=1, keepdims=True)
    ) * image_inverse

    caption_copy.wait_send()
    back_copy.wait_send()
    for d in range(1, groups):
        line_copy(d).wait_send()
        sum_copy(d).wait_send()
    for m in masks:
        for d in range(groups):
            plane_copy(m, d).wait_send()
            part_copy(m, d).wait_send()


def shards(image_embed, caption_vectors, caption_counts, natural_log_multiplier, match_odds_offset):
    image_count, width = image_embed.shape
    slots = caption_vectors.shape[0]
    chips = lax.axis_size("blk") // 2
    groups = lax.axis_size("group")
    blk = lax.axis_index("blk")
    group = lax.axis_index("group")
    scalars = jnp.concatenate([jnp.exp(natural_log_multiplier), match_odds_offset])

    by_device = caption_counts.reshape(-1, image_count)
    own = lax.dynamic_index_in_dim(by_device, blk * groups + group, 0, keepdims=False)
    pair = lax.dynamic_index_in_dim(
        by_device, (blk + 1 - 2 * (blk % 2)) * groups + group, 0, keepdims=False
    )
    totals = jnp.stack([jnp.sum(own), jnp.sum(pair)])
    index = jnp.arange(image_count)
    ends = jnp.sum(jnp.where(index[:, None] <= index[None, :], own[:, None], 0), axis=0)
    bounds = jnp.stack([ends - own, ends])
    mine = jnp.arange(groups * image_count) // image_count == group
    bounds = jnp.where(mine[None, :], jnp.tile(bounds, (1, groups)), 4 * slots)

    vmem = pl.BlockSpec(memory_space=pltpu.VMEM)
    smem = pl.BlockSpec(memory_space=pltpu.SMEM)
    low, full = jnp.bfloat16, jnp.float32
    dma = pltpu.SemaphoreType.DMA
    columns = groups * image_count
    return pl.pallas_call(
        functools.partial(kernel, chips, groups),
        out_shape=(
            jax.ShapeDtypeStruct((image_count, width), full),
            jax.ShapeDtypeStruct((slots, width), full),
        ),
        in_specs=[vmem, vmem, vmem, smem, smem],
        out_specs=(vmem, vmem),
        scratch_shapes=[
            pltpu.VMEM((chips, groups, image_count, width), low),
            pltpu.VMEM((2, slots, width), low),
            pltpu.VMEM((slots, 1), full),
            pltpu.VMEM((2, slots, width), full),
            pltpu.VMEM((columns, width), full),
            pltpu.VMEM((columns, width), full),
            pltpu.VMEM((chips - 1, groups, image_count, width), low),
            pltpu.VMEM((chips - 1, groups, image_count, width), low),
            pltpu.VMEM((groups - 1, image_count, width), low),
            pltpu.VMEM((groups - 1, image_count, width), low),
            pltpu.VMEM((slots, width), low),
            pltpu.VMEM((slots, width), low),
            dma((groups - 1,)), dma((groups - 1,)),
            dma((chips - 1, groups)), dma((chips - 1, groups)),
            dma((chips - 1, groups)), dma((chips - 1, groups)),
            dma((groups - 1,)), dma((groups - 1,)),
            dma((2,)), dma((2,)),
        ],
        compiler_params=pltpu.CompilerParams(collective_id=0, has_side_effects=True),
    )(image_embed, caption_vectors, bounds, totals, scalars)


def solution(mesh):
    placed = (P(("blk", "group"), None), P(("blk", "group"), None), P(), P(), P())
    return jax.shard_map(
        shards,
        mesh=mesh,
        in_specs=placed,
        out_specs=(P(("blk", "group"), None), P(("blk", "group"), None)),
        check_vma=False,
    )
```

time: 276 us -> 82.6 us (0.30)
  waiting for transfers between devices: 166 us -> 0 us
  Pallas kernels: 0 us -> 69.4 us
  local copies, waits for them, and re-layouts: 38.3 us -> 5.77 us
  matrix products: 25.6 us -> 0 us
  other arithmetic: 19.3 us -> 3.86 us
  between operations: 15.7 us -> 2 us
  starting transfers between devices: 9.31 us -> 0 us
    ppermute x9 -> x0, waiting for transfers between devices: 166 us -> none  [the longest x7 147 us: shifted(): return lax.ppermute(block, axis, route)]
    pallas_call x0 -> x1, Pallas kernels: none -> 69.4 us  [shards(): pl.pallas_call(functools.partial(kernel, chips, groups), out_shape=(jax.S...]
    gather x29 -> x0, local copies, waits for them, and re-layouts: 32.3 us -> none
    dot_general x12 -> x0, matrix products: 25.6 us -> none  [the longest x4 10.4 us: row_terms(): jnp.dot(match_loss_factors, gathered, preferred_element_type=jnp.float32)]
    ppermute x9 -> x0, starting transfers between devices: 9.23 us -> none  [the longest x2 4.78 us: swapped(): lax.ppermute(value, axis, [(i, i ^ 1 << stride) for i in range(lax.axis_s...]
    select_n x11 -> x1, other arithmetic: 5.26 us -> 0.58 us  [shards(): bounds = jnp.where(mine[None, :], jnp.tile(bounds, (1, groups)), 4 * slots)]
    reduce_sum x8 -> x2, other arithmetic: 3.92 us -> 0.74 us  [the longest x1 0.65 us: shards(): totals = jnp.stack([jnp.sum(own), jnp.sum(pair)])]
  transfers between devices with their start and end apart: 11 -> 0, of which waited for: 8 -> 0; matrix products, arithmetic and copies ran while one was open for 22% -> 0% of each run, Pallas kernels for 0% -> 0%
where the time goes in v1:
time: 82.6 us; the launch traced here: 81.1 us
  Pallas kernels  69.4 us (84%)
  local copies, waits for them, and re-layouts  5.77 us (7%)
  other arithmetic  3.86 us (5%)
  between operations  2 us (2%)
    pallas_call x1, Pallas kernels, shards(): pl.pallas_call(functools.partial(kernel, chips, groups), out_shape=(jax.S...  69.4 us
    unnamed x2, local copies, waits for them, and re-layouts  4.92 us
    another operation x1, other arithmetic, shards(): totals = jnp.stack([jnp.sum(own), jnp.sum(pair)])  1.87 us

profile of v1, /device:TPU:0, one launch (start us, length us, event | category | flops | bytes accessed | tf_op | source)
XLA Modules:
  0.0 81.1 jit_solution(10617509601917026925)
XLA Ops:
  2.0 0.6 pad_maximum_fusion.scalars_ref
  2.6 0.8 reshape.28
  3.4 0.1 select_reduce_fusion
  3.5 0.6 fusion.1
  4.2 1.9 %pad_add_fusion.1.totals_ref = s32[2]{0:T(128)} fusion(s32[1]{0:T(128)} %bitcast.3, s32[1]{0:T(128)} %bitcast.2), kind=kLoop, calls=%fused_computation.9 | loop fusion | flops 2 | bytes 16 | tf_op jit(solution)/shard_map/stack | solution.py:229
  6.0 0.1 tile.10
  6.1 0.6 broadcast_select_fusion.bounds_ref
  6.7 69.4 %shard_map.68 = (f32[64,1152]{1,0:T(8,128)}, f32[512,1152]{1,0:T(8,128)}) custom-call(bf16[64,1152]{1,0:T(8,128)(2,1)} %image_ref.1, bf16[512,1152]{1,0:T(8,128)(2,1)} %caption_ref.1, s32[2,256]{1,0:T(2,128)} %broadcast_select_fusion.bounds_ref, s32[2]{0:T(128)} %pad_add_fusion.1.totals_ref, f32[2]{0:T(128)} %pad_maximum_fusion.scalars_ref), custom_call_target="tpu_custom_call" | custom-call | tf_op jit(solution)/shard_map/pallas_call | solution.py:241
  76.2 1.7 %copy.11 = f32[64,1152]{1,0:T(8,128)} copy(f32[64,1152]{1,0:T(8,128)} %get-tuple-element.7) | data formatting | bytes 589824
  77.8 3.2 %copy.12 = f32[512,1152]{1,0:T(8,128)} copy(f32[512,1152]{1,0:T(8,128)} %get-tuple-element.8) | data formatting | bytes 4718592
  (4 shorter events, 0.0 us)

commit v2 on v1

--- a/solution.py
+++ b/solution.py
@@ -75,16 +75,34 @@
         here = images.at[chip, group]
         return remote(here, here, line_send.at[d - 1], line_recv.at[d - 1], line_peer(d))
 
+    near = [m for m in masks if bin(m).count("1") == 1]
+    far = [m for m in masks if m not in near]
+
+    def first_hop(mask, index):
+        bits = [b for b in near if b & mask]
+        return bits[index % len(bits)]
+
     def plane_copy(mask, d):
-        here = images.at[chip, (group - d + groups) % groups]
+        first = 0 if mask in near else first_hop(mask, d)
+        here = images.at[flipped(chip, first), (group - d + groups) % groups]
         return remote(
-            here, here, plane_send.at[mask - 1, d], plane_recv.at[mask - 1, d], plane_peer(mask)
+            here, here, plane_send.at[mask - 1, d], plane_recv.at[mask - 1, d],
+            plane_peer(mask - first),
         )
 
+    def relayed(mask):
+        return bin(mask).count("1") == 2
+
+    def joining(mask, unit):
+        return [
+            m for m in far if relayed(m) and mask in near and m - first_hop(m, unit) == mask
+        ]
+
     def part_copy(mask, unit):
+        first = first_hop(mask, unit) if relayed(mask) else mask
         return remote(
             out_partial.at[mask - 1, unit], in_partial.at[mask - 1, unit],
-            part_send.at[mask - 1, unit], part_recv.at[mask - 1, unit], plane_peer(mask),
+            part_send.at[mask - 1, unit], part_recv.at[mask - 1, unit], plane_peer(first),
         )
 
     def sum_copy(d):
@@ -93,11 +111,9 @@
             line_peer(d),
         )
 
-    near = [m for m in masks if bin(m).count("1") == 1]
-    far = [m for m in masks if m not in near]
     for d in range(1, groups):
         line_copy(d).start()
-    for m in masks:
+    for m in near:
         plane_copy(m, 0).start()
 
     step = min(slots, 128)
@@ -116,9 +132,6 @@
     for d in range(1, groups):
         line_copy(d).wait_recv()
         for m in near:
-            plane_copy(m, d).start()
-    for d in range(1, groups):
-        for m in far:
             plane_copy(m, d).start()
     caption_copy.wait_recv()
 
@@ -155,14 +168,31 @@
             )
 
     chunk(chip, own_partial, True)
+    for d in range(groups):
+        for m in near:
+            plane_copy(m, d).wait_recv()
+        for m in far:
+            plane_copy(m, d).start()
     for m in masks:
-        for d in range(groups):
+        for d in range(groups if m in far else 0):
             plane_copy(m, d).wait_recv()
         chunk(flipped(chip, m), partial, False)
         for unit in range(groups):
             rows = slice(unit * image_count, (unit + 1) * image_count)
             out_partial[m - 1, unit] = partial[rows, :].astype(jnp.bfloat16)
-            part_copy(m, unit).start()
+            if not joining(m, unit):
+                part_copy(m, unit).start()
+
+    for unit in range(groups):
+        for m in near:
+            sources = joining(m, unit)
+            if sources:
+                total = out_partial[m - 1, unit].astype(jnp.float32)
+                for source in sources:
+                    part_copy(source, unit).wait_recv()
+                    total = total + in_partial[source - 1, unit].astype(jnp.float32)
+                out_partial[m - 1, unit] = total.astype(jnp.bfloat16)
+                part_copy(m, unit).start()
 
     out_caption[...] = caption_sum[1].astype(jnp.bfloat16)
     back_copy = remote(out_caption, in_caption, pair_send.at[1], pair_recv.at[1], pair_peer)
@@ -172,6 +202,8 @@
         rows = pl.ds(pl.multiple_of(unit * image_count, image_count), image_count)
         total = own_partial[rows, :]
         for m in masks:
+            if relayed(m):
+                continue
             part_copy(m, unit).wait_recv()
             total = total + in_partial[m - 1, unit].astype(jnp.float32)
         return total

time: 82.6 us -> 81.4 us (0.985); the launches traced: 81.1 us -> 81.1 us
  no operation moved by 1% of the time
where the time goes in v2:
time: 81.4 us; the launch traced here: 81.1 us
  Pallas kernels  69.5 us (85%)
  local copies, waits for them, and re-layouts  5.77 us (7%)
  other arithmetic  3.86 us (5%)
  between operations  2 us (2%)
    pallas_call x1, Pallas kernels, shards(): pl.pallas_call(functools.partial(kernel, chips, groups), out_shape=(jax.S...  69.5 us
    unnamed x2, local copies, waits for them, and re-layouts  4.92 us
    another operation x1, other arithmetic, shards(): totals = jnp.stack([jnp.sum(own), jnp.sum(pair)])  1.87 us

profile of v2, /device:TPU:0, one launch (start us, length us, event | category | flops | bytes accessed | tf_op | source)
XLA Modules:
  0.0 81.1 jit_solution(17095813381255098253)
XLA Ops:
  2.0 0.6 pad_maximum_fusion.scalars_ref
  2.6 0.8 reshape.28
  3.4 0.1 select_reduce_fusion
  3.5 0.6 fusion.1
  4.2 1.9 %pad_add_fusion.1.totals_ref = s32[2]{0:T(128)} fusion(s32[1]{0:T(128)} %bitcast.3, s32[1]{0:T(128)} %bitcast.2), kind=kLoop, calls=%fused_computation.9 | loop fusion | flops 2 | bytes 16 | tf_op jit(solution)/shard_map/stack | solution.py:261
  6.0 0.1 tile.10
  6.1 0.6 broadcast_select_fusion.bounds_ref
  6.7 69.5 %shard_map.68 = (f32[64,1152]{1,0:T(8,128)}, f32[512,1152]{1,0:T(8,128)}) custom-call(bf16[64,1152]{1,0:T(8,128)(2,1)} %image_ref.1, bf16[512,1152]{1,0:T(8,128)(2,1)} %caption_ref.1, s32[2,256]{1,0:T(2,128)} %broadcast_select_fusion.bounds_ref, s32[2]{0:T(128)} %pad_add_fusion.1.totals_ref, f32[2]{0:T(128)} %pad_maximum_fusion.scalars_ref), custom_call_target="tpu_custom_call" | custom-call | tf_op jit(solution)/shard_map/pallas_call | solution.py:273
  76.2 1.7 %copy.11 = f32[64,1152]{1,0:T(8,128)} copy(f32[64,1152]{1,0:T(8,128)} %get-tuple-element.7) | data formatting | bytes 589824
  77.9 3.2 %copy.12 = f32[512,1152]{1,0:T(8,128)} copy(f32[512,1152]{1,0:T(8,128)} %get-tuple-element.8) | data formatting | bytes 4718592
  (4 shorter events, 0.0 us)
